TPU v7x, 256 devices: a whole 4x4x8 slice. The times are simulated.
256 devices in a mesh: blk: 64 (over x, y_lo, z), grp: 4 (over y_hi, core).
Axes of the slice: x: 4, y: 4 (y_hi: 2, y_lo: 2; y = y_hi * 2 + y_lo), z: 8, core: 2. Of those that a mesh axis runs over, the one named last changes fastest.
Arguments:
- sources: bfloat16 [65536, 256], P('blk'), may hold values from -64 to 64
- positive: int32 [65536], P('blk'), may hold values from 0 to 65535
- src_part: int32 [65536], P('blk'), may hold values from 0 to 7
- destinations: bfloat16 [65536, 256], P(('blk', 'grp')), may hold values from -8 to 8
- dst_part: int32 [65536], P(('blk', 'grp')), may hold values from 0 to 7
Outputs:
- loss: float32 [65536], P('blk')
All inputs are finite; a program needn't handle non-finite values.
Results may differ from a plain program's by a relative error of at most 0.0003.
Values may be sent and summed in bfloat16 or wider, within the bound.
A program may use at most 192 MiB of HBM per device.

v0:
```python
import jax
import jax.numpy as jnp
from jax import lax
from jax.sharding import Mesh
from jax.sharding import PartitionSpec as P

BLK = ("blk_0", "blk_1", "blk_2")
BLK_GRP = ("blk_0", "blk_1", "blk_2", "grp")
SCALE = 3.0
NEG = -1e30


def joined_along(parts, dim):
    dims = list(parts.shape[1:])
    dims[dim] *= parts.shape[0]
    return jnp.moveaxis(parts, 0, dim).reshape(dims)


def stacked_from(x, axes, order):
    parts = x[None]
    for k in order:
        parts = lax.all_gather(parts, axes[k], axis=0, tiled=True)
    held = [lax.axis_size(axes[k]) for k in reversed(order)]
    parts = parts.reshape(*held, *x.shape)
    turned = sorted(range(len(order)), key=lambda place: order[len(order) - 1 - place])
    return parts.transpose(*turned, *range(len(order), parts.ndim)).reshape(-1, *x.shape)


def whole_of(x, axes, order, dim):
    return joined_along(stacked_from(x, axes, order), dim)


def copy_for_each(x, axis):
    size = lax.axis_size(axis)
    return lax.all_to_all(jnp.broadcast_to(x[None], (size, *x.shape)), axis, 0, 0, tiled=True)


def collected_together(x, axis):
    leaves = jax.tree.leaves(x)
    order = sorted(range(len(leaves)), key=lambda k: -leaves[k].size)
    width = (1, *leaves[order[0]].shape)[-1]
    lines = [
        jnp.pad(leaves[k].reshape(-1), (0, -leaves[k].size % width)).reshape(-1, width)
        for k in order
    ]
    both, at, found = (copy_for_each(jnp.concatenate(lines), axis), 0, {})
    for k, line in zip(order, lines):
        section = both[:, at : at + len(line)].reshape(len(both), -1)
        found[k] = section[:, : leaves[k].size].reshape(-1, *leaves[k].shape)
        at += len(line)
    numbers = iter(range(len(leaves)))
    return jax.tree.map(lambda _: found[next(numbers)], x)


def combined_pairwise(pieces, combine):
    while len(jax.tree.leaves(pieces)[0]) > 1:
        pieces = jax.vmap(combine)(
            *(jax.tree.map(lambda part: part[side::2], pieces) for side in (0, 1))
        )
    return jax.tree.map(lambda part: part[0], pieces)


def joined_all(x, axis, combine):
    pieces = collected_together(x, axis)
    return combined_pairwise(pieces, combine)


def global_columns(count, width, group, groups):
    flat = jnp.arange(count, dtype=jnp.int32)
    return flat // width * (groups * width) + group * width + flat % width


def score_block(carry, sources, positive, src_part, block, block_part, columns):
    maxima, totals, pos_logit = carry
    logits = SCALE * lax.dot_general(
        sources, block, (((1,), (1,)), ((), ())), preferred_element_type=jnp.float32
    )
    is_pos = columns[None, :] == positive[:, None]
    keep = (block_part[None, :] != src_part[:, None]) | is_pos
    masked = jnp.where(keep, logits, NEG)
    new_max = jnp.maximum(maxima, jnp.max(masked, axis=1))
    weights = jnp.where(keep, jnp.exp(masked - new_max[:, None]), 0.0)
    totals = jnp.sum(weights, axis=1)
    pos_logit = jnp.sum(jnp.where(is_pos, logits, 0.0), axis=1)
    return (new_max, totals, pos_logit)


def combine(first, second):
    max_a, sum_a, pos_a = first
    max_b, sum_b, pos_b = second
    top = jnp.maximum(max_a, max_b)
    return (top, sum_a * jnp.exp(max_a - top) + sum_b * jnp.exp(max_b - top), pos_a + pos_b)


def on_device(sources, positive, src_part, destinations, dst_part):
    width = destinations.shape[0]
    count_rows = sources.shape[0]
    groups = lax.axis_size("grp")
    group = lax.axis_index("grp")
    start = (
        jnp.full((count_rows,), NEG, jnp.float32),
        jnp.zeros((count_rows,), jnp.float32),
        jnp.zeros((count_rows,), jnp.float32),
    )
    block = whole_of(destinations, BLK, (1, 0, 2), 0)
    columns = global_columns(block.shape[0], width, group, groups)
    carry = score_block(
        start, sources, positive, src_part, block, whole_of(dst_part, BLK, (1, 0, 2), 0), columns
    )
    maxima, totals, pos_logit = joined_all(carry, "grp", combine)
    return maxima + jnp.log(totals) - pos_logit


def solution(mesh):
    finer = Mesh(
        mesh.devices.reshape(4, 2, 8, mesh.shape["grp"]), ("blk_0", "blk_1", "blk_2", "grp")
    )
    placed = (P(BLK, None), P(BLK), P(BLK), P(BLK_GRP, None), P(BLK_GRP))
    return jax.shard_map(on_device, mesh=finer, in_specs=placed, out_specs=P(BLK), check_vma=False)
```

profile of v0, /device:TPU:1, one launch (start us, length us, event | category | flops | bytes accessed | tf_op | source)
XLA Modules:
  0.0 231.4 jit_solution(11904566351215980522)
XLA Ops:
  6.5 0.0 copy-start
  6.5 0.0 all-gather.7.cloned.1.call-start
  6.5 7.1 %all-gather.1 = bf16[512,256]{1,0:T(8,128)(2,1)} all-gather(bf16[256,256]{1,0:T(8,128)(2,1)} %param.8), channel_id=3, replica_groups=mesh['blk_0'=4,'blk_1'=2,'blk_2'=8,'grp'=4] {'blk_1'}, dimensions={0}, use_global_device_ids=true | all-gather | bytes 393216 | tf_op jit(solution)/shard_map/all_gather | solution.py:22
  13.7 0.0 all-gather.7.cloned.1.call-update
  13.7 0.0 all-gather.9.cloned.1.call-start
  13.7 28.8 %all-gather.7.cloned.1.call-done = bf16[8,256,256]{2,1,0:T(8,128)(2,1)} async-done(((bf16[2,256,256]{2,1,0:T(8,128)(2,1)}), bf16[8,256,256]{2,1,0:T(8,128)(2,1)}) %all-gather.7.cloned.1.call-update) | async-done | bytes 1048592 | tf_op jit(solution)/shard_map/all_gather | solution.py:22
  42.5 0.0 all-gather.9.cloned.1.call-update
  42.5 3.3 %all-gather.2 = s32[2,1,256]{2,1,0:T(1,128)S(1)} all-gather(s32[1,1,256]{2,1,0:T(1,128)} %bitcast.35), channel_id=2, replica_groups=mesh['blk_0'=4,'blk_1'=2,'blk_2'=8,'grp'=4] {'blk_1'}, dimensions={0}, use_global_device_ids=true | all-gather | bytes 3072 | tf_op jit(solution)/shard_map/all_gather | solution.py:22
  45.8 8.1 %all-gather.3 = s32[4,2,256]{2,1,0:T(2,128)S(1)} all-gather(s32[1,2,256]{2,1,0:T(2,128)S(1)} %copy.15), channel_id=1, replica_groups=mesh['blk_0'=4,'blk_1'=2,'blk_2'=8,'grp'=4] {'blk_0'}, dimensions={0}, use_global_device_ids=true | all-gather | bytes 10240 | tf_op jit(solution)/shard_map/all_gather | solution.py:22
  54.0 22.8 %all_gather.20 = s32[64,256]{1,0:T(8,128)S(1)} all-gather(s32[8,256]{1,0:T(8,128)S(1)} %reshape.76), channel_id=1, replica_groups=mesh['blk_0'=4,'blk_1'=2,'blk_2'=8,'grp'=4] {'blk_2'}, dimensions={0}, use_global_device_ids=true | all-gather | bytes 73728 | tf_op jit(solution)/shard_map/all_gather | solution.py:22
  76.8 64.4 %all-gather.9.cloned.1.call-done = bf16[64,256,256]{2,1,0:T(8,128)(2,1)} async-done(((bf16[8,256,256]{2,1,0:T(8,128)(2,1)}), bf16[64,256,256]{2,1,0:T(8,128)(2,1)}) %all-gather.9.cloned.1.call-update) | async-done | bytes 8388624 | tf_op jit(solution)/shard_map/all_gather | solution.py:22
  141.2 7.6 %copy.17 = bf16[4,2,8,256,256]{4,3,2,1,0:T(8,128)(2,1)} copy(bf16[4,2,8,256,256]{4,3,1,0,2:T(8,128)(2,1)} %bitcast.23) | data formatting | bytes 16777216 | tf_op jit(solution)/shard_map/transpose | solution.py:26
  148.8 0.0 copy-start.1
  148.8 0.0 copy-start.2
  148.8 0.0 copy-done
  148.8 28.2 %fusion.1 = (f32[1024]{0:T(1024)S(1)}, f32[1024,16384]{1,0:T(8,128)}) fusion(s32[16384]{0:T(1024)S(1)} %fusion.10, s32[16384]{0:T(1024)S(1)} %bitcast.26, s32[1024]{0:T(1024)} %param.6, s32[1024]{0:T(1024)} %param.7, bf16[1024,256]{1,0:T(8,128)(2,1)S(1)} %copy-done, bf16[16384,256]{1,0:T(8,128)(2,1)} %bitcast.24), kind=kOutput, calls=%fused_computation.5 | convolution fusion | flops 8690596864 | bytes 76165120 | tf_op jit(solution)/shard_map/dot_general | solution.py:75
  177.0 0.0 copy-done.1
  177.0 0.0 copy-done.2
  177.0 36.9 %select_reduce_fusion = (f32[1024]{0:T(1024)S(1)}, f32[1024]{0:T(1024)S(1)}) fusion(f32[1024,16384]{1,0:T(8,128)} %get-tuple-element.13, f32[1024]{0:T(1024)S(1)} %broadcast_maximum_fusion, s32[16384]{0:T(1024)S(1)} %fusion.10, s32[16384]{0:T(1024)S(1)} %bitcast.27, s32[1024]{0:T(1024)S(1)} %copy-done.1, s32[1024]{0:T(1024)S(1)} %copy-done.2), kind=kLoop, calls=%fused_computation.3 | loop fusion | flops 167770112 | bytes 67260416 | tf_op jit(solution)/shard_map/reduce_sum | solution.py:83
  214.0 9.7 %all_to_all.5 = f32[4,3,1024]{2,1,0:T(4,128)S(1)} all-to-all(f32[4,3,1024]{2,1,0:T(4,128)S(1)} %broadcast_in_dim.32), channel_id=1, replica_groups=mesh['blk_0'=4,'blk_1'=2,'blk_2'=8,'grp'=4] {'grp'}, dimensions={0} | all-to-all | bytes 98304 | tf_op jit(solution)/shard_map/all_to_all | solution.py:35
  223.9 0.6 fusion.12
  (20 shorter events, 0.4 us)
Async XLA Ops:
  6.5 142.3 %copy-start = (bf16[1024,256]{1,0:T(8,128)(2,1)S(1)}, bf16[1024,256]{1,0:T(8,128)(2,1)}, u32[]{:S(2)}) copy-start(bf16[1024,256]{1,0:T(8,128)(2,1)} %param.5) | copy-start | bytes 1572868
  6.5 35.9 %all-gather.7.cloned.1.call-start = ((), (), s32[]{:S(2)}) async-start(), calls=%async_computation.1 | async-start | bytes 1310720 | tf_op jit(solution)/shard_map/all_gather | solution.py:22
  13.7 127.6 %all-gather.9.cloned.1.call-start = ((), (), s32[]{:S(2)}) async-start(), calls=%async_computation.2 | async-start | bytes 9437184 | tf_op jit(solution)/shard_map/all_gather | solution.py:22
  148.8 28.2 %copy-start.1 = (s32[1024]{0:T(1024)S(1)}, s32[1024]{0:T(1024)}, u32[]{:S(2)}) copy-start(s32[1024]{0:T(1024)} %param.6) | copy-start | bytes 12292
  148.8 28.2 %copy-start.2 = (s32[1024]{0:T(1024)S(1)}, s32[1024]{0:T(1024)}, u32[]{:S(2)}) copy-start(s32[1024]{0:T(1024)} %param.7) | copy-start | bytes 12292
Sparse Core Ops, SparseCore 0:
  13.8 28.6 all-gather.6
  44.3 96.9 all-gather.8
where the time goes:
time: 232 us; the launch traced here: 231 us
  waiting for transfers between devices  93.2 us (40%)
  blocking collectives  51 us (22%)
  other arithmetic  37.6 us (16%)
  matrix products  28.2 us (12%)
  between operations  13.5 us (6%)
  local copies, waits for them, and re-layouts  7.94 us (3%)
    all_gather x2, waiting for transfers between devices, stacked_from(): parts = lax.all_gather(parts, axes[k], axis=0, tiled=True)  93.1 us
    all_gather x4, blocking collectives, stacked_from(): parts = lax.all_gather(parts, axes[k], axis=0, tiled=True)  41.3 us
    reduce_sum x1, other arithmetic, score_block(): totals = jnp.sum(weights, axis=1)  36.9 us
    dot_general x1, matrix products, score_block(): lax.dot_general(sources, block, (((1,), (1,)), ((), ())), preferred_eleme...  28.2 us
    all_to_all x1, blocking collectives, copy_for_each(): lax.all_to_all(jnp.broadcast_to(x[None], (size, *x.shape)), axis, 0, 0, t...  9.68 us
    transpose x1, local copies, waits for them, and re-layouts, stacked_from(): parts.transpose(*turned, *range(len(order), parts.ndim))  7.58 us
  transfers between devices with their start and end apart: 2, of which 2 were waited for; matrix products, arithmetic and copies ran while one was open for 0% of the time, Pallas kernels for 0%

commit v1 on v0

--- a/solution.py
+++ b/solution.py
@@ -19,7 +19,9 @@
 def stacked_from(x, axes, order):
     parts = x[None]
     for k in order:
-        parts = lax.all_gather(parts, axes[k], axis=0, tiled=True)
+        parts = jnp.concatenate(
+            lax.all_to_all(jnp.stack([parts] * lax.axis_size(axes[k])), axes[k], 0, 0), axis=0
+        )
     held = [lax.axis_size(axes[k]) for k in reversed(order)]
     parts = parts.reshape(*held, *x.shape)
     turned = sorted(range(len(order)), key=lambda place: order[len(order) - 1 - place])

time: 232 us -> 323 us (1.39)
  waiting for transfers between devices: 93.2 us -> 184 us
  between operations: 13.5 us -> 0.12 us
  starting transfers between devices: 0.04 us -> 13.1 us
  local copies, waits for them, and re-layouts: 7.94 us -> 12.8 us
    all_to_all x0 -> x2, waiting for transfers between devices: none -> 184 us  [stacked_from(): lax.all_to_all(jnp.stack([parts] * lax.axis_size(axes[k])), axes[k], 0, 0)]
    all_gather x2 -> x0, waiting for transfers between devices: 93.1 us -> none  [stacked_from(): parts = lax.all_gather(parts, axes[k], axis=0, tiled=True)]
    all_gather x4 -> x0, blocking collectives: 41.3 us -> none  [stacked_from(): parts = lax.all_gather(parts, axes[k], axis=0, tiled=True)]
    all_to_all x0 -> x4, blocking collectives: none -> 32.3 us  [stacked_from(): lax.all_to_all(jnp.stack([parts] * lax.axis_size(axes[k])), axes[k], 0, 0)]
    all_to_all x0 -> x2, starting transfers between devices: none -> 13.1 us  [stacked_from(): lax.all_to_all(jnp.stack([parts] * lax.axis_size(axes[k])), axes[k], 0, 0)]
    all_to_all x1, blocking collectives: 9.68 us -> 18.3 us  [copy_for_each(): lax.all_to_all(jnp.broadcast_to(x[None], (size, *x.shape)), axis, 0, 0, t...]
    transpose x1 -> x0, local copies, waits for them, and re-layouts: 7.58 us -> none  [stacked_from(): parts.transpose(*turned, *range(len(order), parts.ndim))]
    all_to_all x0 -> x1, local copies, waits for them, and re-layouts: none -> 7.57 us  [stacked_from(): lax.all_to_all(jnp.stack([parts] * lax.axis_size(axes[k])), axes[k], 0, 0)]
where the time goes in v1:
time: 323 us; the launch traced here: 322 us
  waiting for transfers between devices  184 us (57%)
  blocking collectives  50.7 us (16%)
  other arithmetic  36.2 us (11%)
  matrix products  25.4 us (8%)
  starting transfers between devices  13.1 us (4%)
  local copies, waits for them, and re-layouts  12.8 us (4%)
    all_to_all x2, waiting for transfers between devices, stacked_from(): lax.all_to_all(jnp.stack([parts] * lax.axis_size(axes[k])), axes[k], 0, 0)  184 us
    reduce_sum x1, other arithmetic, score_block(): totals = jnp.sum(weights, axis=1)  33.8 us
    all_to_all x4, blocking collectives, stacked_from(): lax.all_to_all(jnp.stack([parts] * lax.axis_size(axes[k])), axes[k], 0, 0)  32.3 us
    dot_general x1, matrix products, score_block(): lax.dot_general(sources, block, (((1,), (1,)), ((), ())), preferred_eleme...  25.4 us
    all_to_all x1, blocking collectives, copy_for_each(): lax.all_to_all(jnp.broadcast_to(x[None], (size, *x.shape)), axis, 0, 0, t...  18.3 us
    all_to_all x2, starting transfers between devices, stacked_from(): lax.all_to_all(jnp.stack([parts] * lax.axis_size(axes[k])), axes[k], 0, 0)  13.1 us
    all_to_all x1, local copies, waits for them, and re-layouts, stacked_from(): lax.all_to_all(jnp.stack([parts] * lax.axis_size(axes[k])), axes[k], 0, 0)  7.57 us
  transfers between devices with their start and end apart: 2, of which 2 were waited for; matrix products, arithmetic and copies ran while one was open for 0% of the time, Pallas kernels for 0%

profile of v1, /device:TPU:1, one launch (start us, length us, event | category | flops | bytes accessed | tf_op | source)
XLA Modules:
  0.0 322.5 jit_solution(648658534467998901)
XLA Ops:
  0.0 0.0 copy-start
  0.0 0.8 pad_add_fusion
  0.8 5.8 %all_to_all.35 = s32[2,1,256]{2,1,0:T(1,128)S(1)} all-to-all(s32[2,1,256]{2,1,0:T(1,128)S(1)} %pad_add_fusion), channel_id=1, replica_groups=mesh['blk_0'=4,'blk_1'=2,'blk_2'=8,'grp'=4] {'blk_1'}, dimensions={0} | all-to-all | bytes 4096 | tf_op jit(solution)/shard_map/all_to_all | solution.py:23
  6.6 8.0 %all_to_all.36 = s32[4,2,256]{2,1,0:T(2,128)S(1)} all-to-all(s32[4,2,256]{2,1,0:T(2,128)S(1)} %stack.19), channel_id=1, replica_groups=mesh['blk_0'=4,'blk_1'=2,'blk_2'=8,'grp'=4] {'blk_0'}, dimensions={0} | all-to-all | bytes 16384 | tf_op jit(solution)/shard_map/all_to_all | solution.py:23
  14.6 0.6 stack.20
  15.2 8.2 %all-to-all-start.2 = ((s32[8,8,256]{2,1,0:T(8,128)}), s32[8,8,256]{2,1,0:T(8,128)S(1)}, u32[]{:S(2)}, u32[]{:S(2)}) async-start(s32[8,8,256]{2,1,0:T(8,128)} %stack.20), calls=%async_computation.2 | async-start | bytes 131072 | tf_op jit(solution)/shard_map/all_to_all | solution.py:23
  23.4 1.0 pad_maximum_fusion
  24.4 6.2 %all-to-all-done.2 = s32[8,8,256]{2,1,0:T(8,128)S(1)} async-done(((s32[8,8,256]{2,1,0:T(8,128)}), s32[8,8,256]{2,1,0:T(8,128)S(1)}, u32[]{:S(2)}, u32[]{:S(2)}) %all-to-all-start.2) | async-done | bytes 65568 | tf_op jit(solution)/shard_map/all_to_all | solution.py:23
  30.6 6.4 %all_to_all.37 = bf16[2,1,256,256]{3,2,1,0:T(8,128)(2,1)S(1)} all-to-all(bf16[2,1,256,256]{3,2,1,0:T(8,128)(2,1)S(1)} %pad_maximum_fusion), channel_id=1, replica_groups=mesh['blk_0'=4,'blk_1'=2,'blk_2'=8,'grp'=4] {'blk_1'}, dimensions={0} | all-to-all | bytes 524288 | tf_op jit(solution)/shard_map/all_to_all | solution.py:23
  37.0 0.1 stack.22
  37.1 12.2 %all_to_all.38 = bf16[4,2,256,256]{3,2,1,0:T(8,128)(2,1)S(1)} all-to-all(bf16[4,2,256,256]{3,2,1,0:T(8,128)(2,1)S(1)} %stack.22), channel_id=1, replica_groups=mesh['blk_0'=4,'blk_1'=2,'blk_2'=8,'grp'=4] {'blk_0'}, dimensions={0} | all-to-all | bytes 2097152 | tf_op jit(solution)/shard_map/all_to_all | solution.py:23
  49.2 4.2 %stack.23 = bf16[8,8,256,256]{3,2,1,0:T(8,128)(2,1)} broadcast(bf16[8,256,256]{2,1,0:T(8,128)(2,1)S(1)} %bitcast.40), dimensions={1,2,3} | broadcast | bytes 9437184 | tf_op jit(solution)/shard_map/stack | solution.py:23
  53.5 4.9 %all-to-all-start.5 = ((bf16[8,8,256,256]{3,2,1,0:T(8,128)(2,1)}), bf16[8,8,256,256]{3,2,1,0:T(8,128)(2,1)}, u32[]{:S(2)}, u32[]{:S(2)}) async-start(bf16[8,8,256,256]{3,2,1,0:T(8,128)(2,1)} %stack.23), calls=%async_computation.5 | async-start | bytes 16777216 | tf_op jit(solution)/shard_map/all_to_all | solution.py:23
  58.5 177.8 %all-to-all-done.5 = bf16[8,8,256,256]{3,2,1,0:T(8,128)(2,1)} async-done(((bf16[8,8,256,256]{3,2,1,0:T(8,128)(2,1)}), bf16[8,8,256,256]{3,2,1,0:T(8,128)(2,1)}, u32[]{:S(2)}, u32[]{:S(2)}) %all-to-all-start.5) | async-done | bytes 8388640 | tf_op jit(solution)/shard_map/all_to_all | solution.py:23
  236.4 7.6 %copy.11 = bf16[8,8,256,256]{3,2,0,1:T(8,128)(2,1)} copy(bf16[8,8,256,256]{3,2,1,0:T(8,128)(2,1)} %all-to-all-done.5) | data formatting | bytes 16777216 | tf_op jit(solution)/shard_map/all_to_all | solution.py:23
  243.9 0.0 copy-done
  243.9 0.0 copy-start.1
  243.9 0.0 copy-start.2
  243.9 25.4 %fusion.1 = (f32[1024]{0:T(1024)S(1)}, f32[16384,1024]{1,0:T(8,128)}) fusion(s32[1024]{0:T(1024)} %param.6, s32[1024]{0:T(1024)} %param.7, s32[16384]{0:T(1024)S(1)} %fusion.10, s32[16384]{0:T(1024)S(1)} %bitcast.42, bf16[16384,256]{1,0:T(8,128)(2,1)} %bitcast.39, bf16[1024,256]{1,0:T(8,128)(2,1)S(1)} %copy-done), kind=kOutput, calls=%fused_computation.5 | convolution fusion | flops 8690596864 | bytes 76165120 | tf_op jit(solution)/shard_map/dot_general | solution.py:77
  269.4 0.0 copy-done.1
  269.4 0.0 copy-done.2
  269.4 33.8 %select_reduce_fusion = (f32[1024]{0:T(1024)S(1)}, f32[1024]{0:T(1024)S(1)}) fusion(f32[16384,1024]{1,0:T(8,128)} %get-tuple-element.13, f32[1024]{0:T(1024)S(1)} %broadcast_maximum_fusion, s32[1024]{0:T(1024)S(1)} %copy-done.1, s32[1024]{0:T(1024)S(1)} %copy-done.2, s32[16384]{0:T(1024)S(1)} %fusion.10, s32[16384]{0:T(1024)S(1)} %bitcast.43), kind=kLoop, calls=%fused_computation.4 | loop fusion | flops 167770112 | bytes 67260416 | tf_op jit(solution)/shard_map/reduce_sum | solution.py:85
  303.2 18.3 %all_to_all.39 = f32[4,3,1024]{2,1,0:T(4,128)S(1)} all-to-all(f32[4,3,1024]{2,1,0:T(4,128)S(1)} %broadcast_in_dim.24), channel_id=1, replica_groups=mesh['blk_0'=4,'blk_1'=2,'blk_2'=8,'grp'=4] {'grp'}, dimensions={0} | all-to-all | bytes 98304 | tf_op jit(solution)/shard_map/all_to_all | solution.py:37
  321.8 0.6 fusion.12
  (20 shorter events, 0.4 us)
Async XLA Ops:
  0.0 243.9 %copy-start = (bf16[1024,256]{1,0:T(8,128)(2,1)S(1)}, bf16[1024,256]{1,0:T(8,128)(2,1)}, u32[]{:S(2)}) copy-start(bf16[1024,256]{1,0:T(8,128)(2,1)} %param.5) | copy-start | bytes 1572868
  15.2 15.4 %all-to-all-start.2 = ((s32[8,8,256]{2,1,0:T(8,128)}), s32[8,8,256]{2,1,0:T(8,128)S(1)}, u32[]{:S(2)}, u32[]{:S(2)}) async-start(s32[8,8,256]{2,1,0:T(8,128)} %stack.20), calls=%async_computation.2 | async-start | bytes 131072 | tf_op jit(solution)/shard_map/all_to_all | solution.py:23
  53.5 182.9 %all-to-all-start.5 = ((bf16[8,8,256,256]{3,2,1,0:T(8,128)(2,1)}), bf16[8,8,256,256]{3,2,1,0:T(8,128)(2,1)}, u32[]{:S(2)}, u32[]{:S(2)}) async-start(bf16[8,8,256,256]{3,2,1,0:T(8,128)(2,1)} %stack.23), calls=%async_computation.5 | async-start | bytes 16777216 | tf_op jit(solution)/shard_map/all_to_all | solution.py:23
  243.9 25.5 %copy-start.1 = (s32[1024]{0:T(1024)S(1)}, s32[1024]{0:T(1024)}, u32[]{:S(2)}) copy-start(s32[1024]{0:T(1024)} %param.6) | copy-start | bytes 12292
  243.9 25.5 %copy-start.2 = (s32[1024]{0:T(1024)S(1)}, s32[1024]{0:T(1024)}, u32[]{:S(2)}) copy-start(s32[1024]{0:T(1024)} %param.7) | copy-start | bytes 12292
